TPU v7x, 32 devices: a whole 2x2x4 slice. The times are simulated.
32 devices in a mesh: dp: 4 (over z), tensor: 8 (over y, x, core).
Axes of the slice: x: 2, y: 2, z: 4, core: 2. Of those that a mesh axis runs over, the one named last changes fastest.
Arguments:
- projected: bfloat16 [2, 4096, 4608], P(None, ('dp', 'tensor')), may hold values from -60 to 60
- out_grad: bfloat16 [2, 4096, 4608], P(None, ('dp', 'tensor')), may hold values from -20 to 20
- attention: bfloat16 [2, 4096, 4096], P(None, 'dp', 'tensor'), may hold values from -6 to 6
- w_out: bfloat16 [4096, 4608], P('tensor'), may hold values from -0.09375 to 0.09375
- gains: float32 [4608], replicated, may hold values from 0.5 to 1.5
- main_out: float32 [4096, 4608], P('tensor', 'dp'), may hold values from -6 to 6
- main_gains: float32 [4608], replicated, may hold values from -6 to 6
Outputs:
- attn_grad: bfloat16 [2, 4096, 4096], P(None, 'dp', 'tensor')
- new_main_out: float32 [4096, 4608], P('tensor', 'dp')
- new_main_gains: float32 [4608], replicated
All inputs are finite; a program needn't handle non-finite values.
Results may differ from a plain program's by a relative error of at most 0.0049.
Values may be sent and summed in bfloat16 or wider, within the bound.
A program may use at most 128 MiB of HBM per device.

v0:
```python
import math
import jax
import jax.numpy as jnp
from jax import lax
from jax.sharding import PartitionSpec as P


def normalized(values):
    inverse = lax.rsqrt(jnp.mean(values * values, axis=-1, keepdims=True) + 1e-06)
    return (values * inverse, inverse)


def norm_back(upstream, normed, inverse):
    return inverse * (upstream - normed * jnp.mean(upstream * normed, axis=-1, keepdims=True))


def per_device(projected, out_grad, attention, w_out, gains, main_out, main_gains):
    micro_count = projected.shape[0]
    own_rows = projected.shape[1]
    tokens_all = micro_count * own_rows * lax.axis_size("dp") * lax.axis_size("tensor")
    factor = 1.0 / math.sqrt(tokens_all)
    gain_total = jnp.zeros(gains.shape, jnp.float32)
    back_list = []
    for micro_step in range(micro_count):
        output_in = projected[micro_step].astype(jnp.float32)
        upstream = out_grad[micro_step].astype(jnp.float32)
        out_hat, out_inv = normalized(output_in)
        out_gain = jnp.sum(upstream * out_hat, axis=0)
        out_back = norm_back(upstream * gains, out_hat, out_inv).astype(jnp.bfloat16)
        back_list.append(out_back)
        gain_total = gain_total + lax.psum(out_gain, ("dp", "tensor"))
    stacked = jnp.stack(back_list)
    section = lax.all_gather(stacked, "tensor", axis=1, tiled=True)
    weight_sum = lax.dot_general(
        attention, section, (((0, 1), (0, 1)), ((), ())), preferred_element_type=jnp.float32
    )
    product = lax.dot_general(
        section, w_out, (((2,), (1,)), ((), ())), preferred_element_type=jnp.float32
    ).astype(jnp.bfloat16)
    shard_out = lax.psum_scatter(weight_sum, "dp", scatter_dimension=1, tiled=True)
    return (product, main_out + factor * shard_out, main_gains + factor * gain_total)


def solution(mesh):
    placed = (
        P(None, ("dp", "tensor"), None),
        P(None, ("dp", "tensor"), None),
        P(None, "dp", "tensor"),
        P("tensor", None),
        P(),
        P("tensor", "dp"),
        P(),
    )
    return jax.shard_map(
        per_device,
        mesh=mesh,
        in_specs=placed,
        out_specs=(P(None, "dp", "tensor"), P("tensor", "dp"), P()),
        check_vma=False,
    )
```

profile of v0, /device:TPU:0, one launch (start us, length us, event | category | flops | bytes accessed | tf_op | source)
XLA Modules:
  0.0 310.6 jit_solution(4926830392892736923)
XLA Ops:
  7.2 0.0 copy-start
  7.2 0.0 all-gather.2.cloned.1.call-start
  7.2 0.0 copy-start.1
  7.2 2.3 fusion.22
  9.6 0.2 copy-done.1
  9.7 0.0 copy-start.2
  9.7 0.0 copy-start.3
  9.7 3.5 %fusion.13 = (f32[128]{0:T(128)S(1)}, f32[128]{0:T(128)S(1)}, f32[4608]{0:T(1024)S(1)}, f32[4608]{0:T(1024)S(1)}) fusion(f32[128]{0:T(128)S(1)} %get-tuple-element.15, f32[4608]{0:T(1024)} %param.11, bf16[2,128,4608]{2,1,0:T(8,128)(2,1)} %param.8, bf16[2,128,4608]{2,1,0:T(8,128)(2,1)S(1)} %copy-done.1, f32[128]{0:T(128)S(1)} %get-tuple-element.14), kind=kLoop, calls=%fused_computation.22 | loop fusion | flops 9427712 | bytes 4775936 | tf_op jit(solution)/shard_map/reduce_sum | solution.py:14
  13.2 0.0 copy-done.2
  13.2 0.0 copy-done.3
  13.2 1.4 fusion.17
  14.7 1.6 pad_maximum_fusion
  16.3 0.0 all-gather.2.cloned.1.call-update
  16.3 0.0 reduce-scatter.2.cloned.1.call-start
  16.4 101.4 %all-gather.2.cloned.1.call-done = bf16[2,1024,4608]{2,1,0:T(8,128)(2,1)} async-done(((bf16[2,128,4608]{2,1,0:T(8,128)(2,1)}), bf16[2,1024,4608]{2,1,0:T(8,128)(2,1)}) %all-gather.2.cloned.1.call-update) | async-done | bytes 18874384 | tf_op jit(solution)/shard_map/all_gather | solution.py:33
  117.8 0.0 copy-done
  117.8 16.1 %convolution_bitcast_fusion = f32[512,4608]{0,1:T(8,128)} fusion(bf16[2,1024,4608]{2,1,0:T(8,128)(2,1)} %all-gather.2.cloned.1.call-done, bf16[2,1024,512]{2,1,0:T(8,128)(2,1)S(1)} %copy-done), kind=kOutput, calls=%fused_computation | convolution fusion | flops 9663676416 | bytes 30408704 | tf_op jit(solution)/shard_map/dot_general | solution.py:34
  133.9 0.0 reduce-scatter.2.cloned.1.call-update
  134.0 0.0 copy-start.4
  134.0 3.0 copy.11
  137.0 46.6 %psum.16 = f32[4608]{0:T(1024)S(1)} all-reduce(f32[4608]{0:T(1024)S(1)} %add.34), channel_id=1, replica_groups=mesh['dp'=4,'tensor'=8] {'dp','tensor'}, use_global_device_ids=true, to_apply=%region_6.0 | all-reduce | flops 4608 | bytes 36864 | tf_op jit(solution)/shard_map/psum | solution.py:31
  183.6 0.0 copy-done.4
  183.6 0.6 multiply_add_fusion.1
  184.2 16.2 %fusion.26 = bf16[2,1024,512]{2,1,0:T(8,128)(2,1)} fusion(bf16[2,1024,4608]{2,1,0:T(8,128)(2,1)} %all-gather.2.cloned.1.call-done, bf16[512,4608]{1,0:T(8,128)(2,1)} %param.10), kind=kOutput, calls=%fused_computation.37 | convolution fusion | flops 9664724992 | bytes 25690112 | tf_op jit(solution)/shard_map/dot_general | solution.py:37
  200.4 95.9 %reduce-scatter.2.cloned.1.call-done = f32[512,1152]{0,1:T(8,128)} async-done(((f32[512,4608]{0,1:T(8,128)}), f32[512,1152]{0,1:T(8,128)}) %reduce-scatter.2.cloned.1.call-update) | async-done | bytes 2359312 | tf_op jit(solution)/shard_map/reduce_scatter | solution.py:40
  296.4 4.3 %multiply_add_fusion = f32[512,1152]{0,1:T(8,128)} fusion(f32[512,1152]{0,1:T(8,128)} %copy.11, f32[512,1152]{0,1:T(8,128)} %reduce-scatter.2.cloned.1.call-done), kind=kLoop, calls=%fused_computation.36 | loop fusion | flops 1179648 | bytes 7077888 | tf_op jit(solution)/shard_map/add | solution.py:41
  300.7 3.0 copy.12
  (4 shorter events, 0.0 us)
Async XLA Ops:
  7.2 110.6 %copy-start = (bf16[2,1024,512]{2,1,0:T(8,128)(2,1)S(1)}, bf16[2,1024,512]{2,1,0:T(8,128)(2,1)}, u32[]{:S(2)}) copy-start(bf16[2,1024,512]{2,1,0:T(8,128)(2,1)} %param.9) | copy-start | bytes 6291460
  7.2 110.6 %all-gather.2.cloned.1.call-start = ((), (), s32[]{:S(2)}) async-start(), calls=%async_computation.1 | async-start | bytes 21233664 | tf_op jit(solution)/shard_map/all_gather | solution.py:33
  7.2 2.5 copy-start.1
  9.7 3.5 %copy-start.2 = (bf16[2,128,4608]{2,1,0:T(8,128)(2,1)S(1)}, bf16[2,128,4608]{2,1,0:T(8,128)(2,1)}, u32[]{:S(2)}) copy-start(bf16[2,128,4608]{2,1,0:T(8,128)(2,1)} %param.8) | copy-start | bytes 7077892
  9.7 3.5 %copy-start.3 = (f32[4608]{0:T(1024)S(1)}, f32[4608]{0:T(1024)}, u32[]{:S(2)}) copy-start(f32[4608]{0:T(1024)} %param.11) | copy-start | bytes 55300
  16.3 280.0 %reduce-scatter.2.cloned.1.call-start = ((), (), s32[]{:S(2)}) async-start(), calls=%async_computation.2 | async-start | bytes 11796480 | tf_op jit(solution)/shard_map/reduce_scatter | solution.py:40
  134.0 49.6 %copy-start.4 = (f32[4608]{0:T(1024)S(1)}, f32[4608]{0:T(1024)}, u32[]{:S(2)}) copy-start(f32[4608]{0:T(1024)} %param.13) | copy-start | bytes 55300
Sparse Core Ops, SparseCore 0:
  16.4 101.3 all-gather.1
  134.1 162.2 reduce-scatter.1
where the time goes:
time: 311 us
  waiting for transfers between devices  197 us (63%)
  blocking collectives  46.6 us (15%)
  matrix products  32.4 us (10%)
  between operations  14.1 us (5%)
  other arithmetic  13.8 us (4%)
  local copies, waits for them, and re-layouts  6.29 us (2%)
    all_gather x1, waiting for transfers between devices, per_device(): section = lax.all_gather(stacked, 'tensor', axis=1, tiled=True)  101 us
    reduce_scatter x1, waiting for transfers between devices, per_device(): lax.psum_scatter(weight_sum, 'dp', scatter_dimension=1, tiled=True)  95.9 us
    psum x1, blocking collectives, per_device(): gain_total = gain_total + lax.psum(out_gain, ('dp', 'tensor'))  46.6 us
    dot_general x1, matrix products, per_device(): lax.dot_general(section, w_out, (((2,), (1,)), ((), ())), preferred_eleme...  16.2 us
    dot_general x1, matrix products, per_device(): lax.dot_general(attention, section, (((0, 1), (0, 1)), ((), ())), preferr...  16.1 us
    unnamed x12, local copies, waits for them, and re-layouts  6.29 us
  transfers between devices with their start and end apart: 2, of which 2 were waited for; matrix products, arithmetic and copies ran while one was open for 6% of the time, Pallas kernels for 0%

commit v1 on v0

--- a/solution.py
+++ b/solution.py
@@ -28,7 +28,7 @@
         out_gain = jnp.sum(upstream * out_hat, axis=0)
         out_back = norm_back(upstream * gains, out_hat, out_inv).astype(jnp.bfloat16)
         back_list.append(out_back)
-        gain_total = gain_total + lax.psum(out_gain, ("dp", "tensor"))
+        gain_total = gain_total + lax.psum(lax.psum(out_gain, "tensor"), "dp")
     stacked = jnp.stack(back_list)
     section = lax.all_gather(stacked, "tensor", axis=1, tiled=True)
     weight_sum = lax.dot_general(

time: 311 us -> 311 us (level)
    psum x1 -> x2, blocking collectives: 46.6 us -> 45.6 us  [per_device(): gain_total = gain_total + lax.psum(lax.psum(out_gain, 'tensor'), 'dp')]
where the time goes in v1:
time: 311 us
  waiting for transfers between devices  198 us (64%)
  blocking collectives  45.6 us (15%)
  matrix products  32.4 us (10%)
  between operations  14.1 us (5%)
  other arithmetic  13.8 us (4%)
  local copies, waits for them, and re-layouts  6.29 us (2%)
    all_gather x1, waiting for transfers between devices, per_device(): section = lax.all_gather(stacked, 'tensor', axis=1, tiled=True)  101 us
    reduce_scatter x1, waiting for transfers between devices, per_device(): lax.psum_scatter(weight_sum, 'dp', scatter_dimension=1, tiled=True)  96.8 us
    psum x2, blocking collectives, per_device(): gain_total = gain_total + lax.psum(lax.psum(out_gain, 'tensor'), 'dp')  45.6 us
    dot_general x1, matrix products, per_device(): lax.dot_general(section, w_out, (((2,), (1,)), ((), ())), preferred_eleme...  16.2 us
    dot_general x1, matrix products, per_device(): lax.dot_general(attention, section, (((0, 1), (0, 1)), ((), ())), preferr...  16.1 us
    unnamed x12, local copies, waits for them, and re-layouts  6.29 us
  transfers between devices with their start and end apart: 2, of which 2 were waited for; matrix products, arithmetic and copies ran while one was open for 6% of the time, Pallas kernels for 0%

profile of v1, /device:TPU:0, one launch (start us, length us, event | category | flops | bytes accessed | tf_op | source)
XLA Modules:
  0.0 310.6 jit_solution(17687211353584339173)
XLA Ops:
  7.2 0.0 copy-start
  7.2 0.0 all-gather.2.cloned.1.call-start
  7.2 0.0 copy-start.1
  7.2 2.3 fusion.22
  9.6 0.2 copy-done.1
  9.7 0.0 copy-start.2
  9.7 0.0 copy-start.3
  9.7 3.5 %fusion.13 = (f32[128]{0:T(128)S(1)}, f32[128]{0:T(128)S(1)}, f32[4608]{0:T(1024)S(1)}, f32[4608]{0:T(1024)S(1)}) fusion(f32[128]{0:T(128)S(1)} %get-tuple-element.15, f32[4608]{0:T(1024)} %param.11, bf16[2,128,4608]{2,1,0:T(8,128)(2,1)} %param.8, bf16[2,128,4608]{2,1,0:T(8,128)(2,1)S(1)} %copy-done.1, f32[128]{0:T(128)S(1)} %get-tuple-element.14), kind=kLoop, calls=%fused_computation.22 | loop fusion | flops 9427712 | bytes 4775936 | tf_op jit(solution)/shard_map/reduce_sum | solution.py:14
  13.2 0.0 copy-done.2
  13.2 0.0 copy-done.3
  13.2 1.4 fusion.17
  14.7 1.6 pad_maximum_fusion
  16.3 0.0 all-gather.2.cloned.1.call-update
  16.3 0.0 reduce-scatter.2.cloned.1.call-start
  16.4 101.4 %all-gather.2.cloned.1.call-done = bf16[2,1024,4608]{2,1,0:T(8,128)(2,1)} async-done(((bf16[2,128,4608]{2,1,0:T(8,128)(2,1)}), bf16[2,1024,4608]{2,1,0:T(8,128)(2,1)}) %all-gather.2.cloned.1.call-update) | async-done | bytes 18874384 | tf_op jit(solution)/shard_map/all_gather | solution.py:33
  117.8 0.0 copy-done
  117.8 16.1 %convolution_bitcast_fusion = f32[512,4608]{0,1:T(8,128)} fusion(bf16[2,1024,4608]{2,1,0:T(8,128)(2,1)} %all-gather.2.cloned.1.call-done, bf16[2,1024,512]{2,1,0:T(8,128)(2,1)S(1)} %copy-done), kind=kOutput, calls=%fused_computation | convolution fusion | flops 9663676416 | bytes 30408704 | tf_op jit(solution)/shard_map/dot_general | solution.py:34
  133.9 0.0 reduce-scatter.2.cloned.1.call-update
  134.0 0.0 copy-start.4
  134.0 3.0 copy.11
  137.0 24.7 %psum.33 = f32[4608]{0:T(1024)S(1)} all-reduce(f32[4608]{0:T(1024)S(1)} %add.38), channel_id=1, replica_groups=mesh['dp'=4,'tensor'=8] {'tensor'}, use_global_device_ids=true, to_apply=%region_6.0 | all-reduce | flops 4608 | bytes 36864 | tf_op jit(solution)/shard_map/psum | solution.py:31
  161.7 21.0 %psum.32 = f32[4608]{0:T(1024)S(1)} all-reduce(f32[4608]{0:T(1024)S(1)} %psum.33), channel_id=1, replica_groups=mesh['dp'=4,'tensor'=8] {'dp'}, use_global_device_ids=true, to_apply=%region_7.0 | all-reduce | flops 4608 | bytes 36864 | tf_op jit(solution)/shard_map/psum | solution.py:31
  182.7 0.0 copy-done.4
  182.7 0.6 multiply_add_fusion.1
  183.3 16.2 %fusion.26 = bf16[2,1024,512]{2,1,0:T(8,128)(2,1)} fusion(bf16[2,1024,4608]{2,1,0:T(8,128)(2,1)} %all-gather.2.cloned.1.call-done, bf16[512,4608]{1,0:T(8,128)(2,1)} %param.10), kind=kOutput, calls=%fused_computation.37 | convolution fusion | flops 9664724992 | bytes 25690112 | tf_op jit(solution)/shard_map/dot_general | solution.py:37
  199.5 96.8 %reduce-scatter.2.cloned.1.call-done = f32[512,1152]{0,1:T(8,128)} async-done(((f32[512,4608]{0,1:T(8,128)}), f32[512,1152]{0,1:T(8,128)}) %reduce-scatter.2.cloned.1.call-update) | async-done | bytes 2359312 | tf_op jit(solution)/shard_map/reduce_scatter | solution.py:40
  296.3 4.3 %multiply_add_fusion = f32[512,1152]{0,1:T(8,128)} fusion(f32[512,1152]{0,1:T(8,128)} %copy.11, f32[512,1152]{0,1:T(8,128)} %reduce-scatter.2.cloned.1.call-done), kind=kLoop, calls=%fused_computation.36 | loop fusion | flops 1179648 | bytes 7077888 | tf_op jit(solution)/shard_map/add | solution.py:41
  300.7 3.0 copy.12
  (4 shorter events, 0.0 us)
Async XLA Ops:
  7.2 110.6 %copy-start = (bf16[2,1024,512]{2,1,0:T(8,128)(2,1)S(1)}, bf16[2,1024,512]{2,1,0:T(8,128)(2,1)}, u32[]{:S(2)}) copy-start(bf16[2,1024,512]{2,1,0:T(8,128)(2,1)} %param.9) | copy-start | bytes 6291460
  7.2 110.6 %all-gather.2.cloned.1.call-start = ((), (), s32[]{:S(2)}) async-start(), calls=%async_computation.1 | async-start | bytes 21233664 | tf_op jit(solution)/shard_map/all_gather | solution.py:33
  7.2 2.5 copy-start.1
  9.7 3.5 %copy-start.2 = (bf16[2,128,4608]{2,1,0:T(8,128)(2,1)S(1)}, bf16[2,128,4608]{2,1,0:T(8,128)(2,1)}, u32[]{:S(2)}) copy-start(bf16[2,128,4608]{2,1,0:T(8,128)(2,1)} %param.8) | copy-start | bytes 7077892
  9.7 3.5 %copy-start.3 = (f32[4608]{0:T(1024)S(1)}, f32[4608]{0:T(1024)}, u32[]{:S(2)}) copy-start(f32[4608]{0:T(1024)} %param.11) | copy-start | bytes 55300
  16.3 280.0 %reduce-scatter.2.cloned.1.call-start = ((), (), s32[]{:S(2)}) async-start(), calls=%async_computation.2 | async-start | bytes 11796480 | tf_op jit(solution)/shard_map/reduce_scatter | solution.py:40
  134.0 48.7 %copy-start.4 = (f32[4608]{0:T(1024)S(1)}, f32[4608]{0:T(1024)}, u32[]{:S(2)}) copy-start(f32[4608]{0:T(1024)} %param.13) | copy-start | bytes 55300
Sparse Core Ops, SparseCore 0:
  16.4 101.3 all-gather.1
  134.1 162.2 reduce-scatter.1
